TPU v7x, 32 devices: a whole 2x2x4 slice. The times are simulated.
32 devices in a mesh: row: 8 (over y, x, core), col: 4 (over z).
Axes of the slice: x: 2, y: 2, z: 4, core: 2. Of those that a mesh axis runs over, the one named last changes fastest.
Arguments:
- vectors: float32 [16384, 16384], P('row', 'col'), may hold values from -0.046875 to 0.046875
- basis: float32 [16384, 2048], P('col', 'row'), may hold values from -9 to 9
- block_units: int32 [8], replicated, may hold values from 1 to 40, 64 in all
Outputs:
- assembled: float32 [16384, 2048], P('row', 'col')
Inputs may be any that keep to these rules, and one draw needn't show every extreme that they name: `block_units`: the block sizes are whole numbers of units that sum to 64; the largest is exactly the maximum.
All inputs are finite; a program needn't handle non-finite values.
Results may differ from a plain program's by a relative error of at most 0.00007.
Values sent between devices are 32-bit elements; how exact they have to be, the bound alone decides.
A program may use at most 192 MiB of HBM per device.

v0:
```python
import jax
import jax.numpy as jnp
from jax import lax
from jax.sharding import PartitionSpec as P

UNIT = 256
START = 7168
LANES = 128


def block_ids(positions, block_units):
    ends = jnp.cumsum(block_units) * UNIT
    return jnp.sum((positions[:, None] >= ends[None, :-1]).astype(jnp.int32), axis=1)


def shards(vectors, basis, block_units):
    inner, width = basis.shape
    row_block = block_ids(
        lax.axis_index("col") * inner + jnp.arange(inner, dtype=jnp.int32), block_units
    )
    slab_block = block_ids(
        START + lax.axis_index("row") * width + jnp.arange(width, dtype=jnp.int32), block_units
    )
    masked = jnp.where(row_block[:, None] == slab_block[None, :], basis, jnp.float32(0.0))

    rows, cols = lax.axis_size("row"), lax.axis_size("col")
    step = LANES if width % LANES == 0 and rows % cols == 0 else width
    pieces = [
        lax.all_gather(masked[:, at:at + step], "row", axis=1, tiled=True)
        for at in range(0, width, step)
    ]
    sums = []
    for piece in pieces:
        part = jnp.dot(
            vectors, piece, precision=lax.Precision.HIGH, preferred_element_type=jnp.float32
        )
        sums.append(lax.psum_scatter(part, "col", scatter_dimension=1, tiled=True))
    groups = sums[0].shape[1] // step
    return jnp.concatenate(
        [one[:, g * step:(g + 1) * step] for g in range(groups) for one in sums], axis=1
    )


def solution(mesh):
    in_specs = (P("row", "col"), P("col", "row"), P())
    out_specs = P("row", "col")
    return jax.shard_map(shards, mesh=mesh, in_specs=in_specs, out_specs=out_specs, check_vma=False)
```

profile of v0, /device:TPU:7, one launch (start us, length us, event | category | flops | bytes accessed | tf_op | source)
XLA Modules:
  0.0 527.0 jit_solution(5976717857978838351)
XLA Ops:
  6.5 0.0 all-gather.3.cloned.1.call-start
  6.5 0.8 reduce-window.9
  7.4 0.1 convert_reduce_fusion.1
  7.5 0.1 convert_reduce_fusion
  7.6 3.9 compare_select_fusion
  11.5 2.3 fusion
  13.8 0.0 all-gather.3.cloned.1.call-update
  13.9 0.0 all-gather.5.cloned.1.call-start
  13.9 0.7 all-gather.5.cloned.1.call-update
  14.6 0.0 reduce-scatter.3.cloned.1.call-start
  14.7 93.1 %all-gather.3.cloned.1.call-done = f32[4096,1024]{1,0:T(8,128)} async-done(((f32[4096,128]{1,0:T(8,128)}), f32[4096,1024]{1,0:T(8,128)}) %all-gather.3.cloned.1.call-update) | async-done | bytes 16777232 | tf_op jit(solution)/shard_map/all_gather | solution.py:29
  107.7 111.0 %convolution_bitcast_fusion.1 = f32[2048,1024]{0,1:T(8,128)} fusion(f32[4096,1024]{1,0:T(8,128)} %all-gather.3.cloned.1.call-done, f32[2048,4096]{1,0:T(8,128)} %param.3), kind=kOutput, calls=%fused_computation.1 | convolution fusion | flops 51539607552 | bytes 58720256 | tf_op jit(solution)/shard_map/dot_general | solution.py:34
  218.7 0.0 reduce-scatter.3.cloned.1.call-update
  218.7 0.0 reduce-scatter.5.cloned.1.call-start
  218.8 0.0 all-gather.5.cloned.1.call-done
  218.8 111.1 %convolution_bitcast_fusion = f32[2048,1024]{0,1:T(8,128)} fusion(f32[4096,1024]{1,0:T(8,128)} %all-gather.5.cloned.1.call-done, f32[2048,4096]{1,0:T(8,128)} %param.3), kind=kOutput, calls=%fused_computation | convolution fusion | flops 51539607552 | bytes 58720256 | tf_op jit(solution)/shard_map/dot_general | solution.py:34
  329.9 0.0 reduce-scatter.5.cloned.1.call-update
  330.0 33.6 %reduce-scatter.3.cloned.1.call-done = f32[2048,256]{0,1:T(8,128)} async-done(((f32[2048,1024]{0,1:T(8,128)}), f32[2048,256]{0,1:T(8,128)}) %reduce-scatter.3.cloned.1.call-update) | async-done | bytes 2097168 | tf_op jit(solution)/shard_map/reduce_scatter | solution.py:37
  363.6 1.7 fusion.1
  365.3 145.8 %reduce-scatter.5.cloned.1.call-done = f32[2048,256]{0,1:T(8,128)} async-done(((f32[2048,1024]{0,1:T(8,128)}), f32[2048,256]{0,1:T(8,128)}) %reduce-scatter.5.cloned.1.call-update) | async-done | bytes 2097168 | tf_op jit(solution)/shard_map/reduce_scatter | solution.py:37
  511.1 1.8 fusion.2
  512.8 2.3 pad_maximum_fusion
  515.2 5.3 %copy.5 = f32[2048,512]{1,0:T(8,128)} copy(f32[2048,512]{0,1:T(8,128)} %pad_maximum_fusion) | data formatting | bytes 8388608 | tf_op jit(solution)/shard_map/concatenate | solution.py:39
  (4 shorter events, 0.0 us)
Async XLA Ops:
  6.5 101.2 %all-gather.3.cloned.1.call-start = ((), (), s32[]{:S(2)}) async-start(), calls=%async_computation.2 | async-start | bytes 18874368 | tf_op jit(solution)/shard_map/all_gather | solution.py:29
  13.9 204.9 %all-gather.5.cloned.1.call-start = ((), (), s32[]{:S(2)}) async-start(), calls=%async_computation.4 | async-start | bytes 18874368 | tf_op jit(solution)/shard_map/all_gather | solution.py:29
  14.6 349.0 %reduce-scatter.3.cloned.1.call-start = ((), (), s32[]{:S(2)}) async-start(), calls=%async_computation.3 | async-start | bytes 10485760 | tf_op jit(solution)/shard_map/reduce_scatter | solution.py:37
  218.7 292.4 %reduce-scatter.5.cloned.1.call-start = ((), (), s32[]{:S(2)}) async-start(), calls=%async_computation.5 | async-start | bytes 10485760 | tf_op jit(solution)/shard_map/reduce_scatter | solution.py:37
Sparse Core Ops, SparseCore 0:
  14.0 93.6 all-gather.2
  109.6 93.0 all-gather.4
  218.8 144.7 reduce-scatter.2
  365.8 145.2 reduce-scatter.4
where the time goes:
time: 529 us; the launch traced here: 527 us
  waiting for transfers between devices  273 us (52%)
  matrix products  222 us (42%)
  between operations  13.2 us (2%)
  local copies, waits for them, and re-layouts  11.1 us (2%)
  other arithmetic  7.3 us (1%)
    dot_general x2, matrix products, shards(): jnp.dot(vectors, piece, precision=lax.Precision.HIGH, preferred_element_t...  222 us
    reduce_scatter x2, waiting for transfers between devices, shards(): sums.append(lax.psum_scatter(part, 'col', scatter_dimension=1, tiled=True))  179 us
    all_gather x2, waiting for transfers between devices, shards(): lax.all_gather(masked[:, at:at + step], 'row', axis=1, tiled=True)  93.1 us
  transfers between devices with their start and end apart: 4, of which 3 were waited for; matrix products, arithmetic and copies ran while one was open for 42% of the time, Pallas kernels for 0%

commit v1 on v0

--- a/solution.py
+++ b/solution.py
@@ -1,11 +1,20 @@
+import functools
+
 import jax
 import jax.numpy as jnp
 from jax import lax
+from jax.experimental import pallas as pl
+from jax.experimental.pallas import tpu as pltpu
 from jax.sharding import PartitionSpec as P
 
 UNIT = 256
 START = 7168
 LANES = 128
+PIECE = 512
+STAGE = 64
+LAG = 4
+VMEM_BYTES = 67043328
+MESH = pl.DeviceIdType.MESH
 
 
 def block_ids(positions, block_units):
@@ -13,7 +22,7 @@
     return jnp.sum((positions[:, None] >= ends[None, :-1]).astype(jnp.int32), axis=1)
 
 
-def shards(vectors, basis, block_units):
+def plain(vectors, basis, block_units):
     inner, width = basis.shape
     row_block = block_ids(
         lax.axis_index("col") * inner + jnp.arange(inner, dtype=jnp.int32), block_units
@@ -41,7 +50,375 @@
     )
 
 
+def pick(at, values):
+    out = values[-1]
+    for i in range(len(values) - 2, -1, -1):
+        out = jnp.where(at == i, values[i], out)
+    return out
+
+
+def kernel(rows, cols, blocks, units_ref, v_ref, b_ref, out_ref, gath, in_r, in_l,
+           vh, vl, part, vst, mst, mh, ml, held,
+           v_sem, m_sem, h_sem, o_sem, link_send, link_recv, twin_send, twin_recv,
+           z_send, right_recv, left_recv):
+    row, c = lax.axis_index("row"), lax.axis_index("col")
+    last = cols - 1
+    core = row % 2
+    chip = row // 2
+    x, y = chip % 2, chip // 2
+    chip_x = y * 2 + (1 - x)
+    chip_y = (1 - y) * 2 + x
+    chip_d = (1 - y) * 2 + (1 - x)
+    twin = chip * 2 + (1 - core)
+    mrows, inner = v_ref.shape
+    per_block = 2 * rows // cols
+    pieces = mrows // PIECE
+    chunks = rows
+    slots = (cols - 1) * per_block
+
+    peer = [
+        None,
+        jnp.where(core == 0, chip_x, chip_y) * 2 + core,
+        jnp.where(core == 0, chip_y, chip_x) * 2 + core,
+        jnp.where(core == 0, chip_x, chip_y) * 2 + core,
+    ]
+
+    def unit_a(q):
+        ph, h = q // 2, q % 2
+        return 2 * pick(ph, [row, chip_x * 2, chip_x * 2 + 1, chip_d * 2 + core]) + h
+
+    def unit_b(q):
+        ph, h = q // 2, q % 2
+        return 2 * pick(ph, [twin, chip_y * 2 + 1, chip_y * 2, chip_d * 2 + (1 - core)]) + h
+
+    def unit_mine(q):
+        ph, h = q // 2, q % 2
+        return 2 * pick(ph, [row, peer[1], peer[2], chip_d * 2 + (1 - core)]) + h
+
+    def own_cols(h):
+        return b_ref.at[:, pl.ds(pl.multiple_of(h * LANES, LANES), LANES)]
+
+    def link_copy(ph, h):
+        q = 2 * ph + h
+        u = 2 * row + h
+        if ph == 3:
+            u = 2 * jnp.where(core == 0, chip_y * 2 + 1, chip_x * 2) + h
+        return pltpu.make_async_remote_copy(
+            src_ref=gath.at[u] if ph == 3 else own_cols(h), dst_ref=gath.at[u],
+            send_sem=link_send.at[q], recv_sem=link_recv.at[q],
+            device_id=(peer[ph], c), device_id_type=MESH)
+
+    def link_arrival(q):
+        u = unit_mine(q)
+        return pltpu.make_async_remote_copy(
+            src_ref=gath.at[u], dst_ref=gath.at[u],
+            send_sem=link_send.at[q], recv_sem=link_recv.at[q],
+            device_id=(twin, c), device_id_type=MESH)
+
+    def twin_own(h):
+        return pltpu.make_async_remote_copy(
+            src_ref=own_cols(h), dst_ref=gath.at[2 * row + h],
+            send_sem=twin_send.at[h], recv_sem=twin_recv.at[h],
+            device_id=(twin, c), device_id_type=MESH)
+
+    def twin_copy(q):
+        u = unit_mine(q)
+        return pltpu.make_async_remote_copy(
+            src_ref=gath.at[u], dst_ref=gath.at[u],
+            send_sem=twin_send.at[q], recv_sem=twin_recv.at[q],
+            device_id=(twin, c), device_id_type=MESH)
+
+    def z_copy(u, s, right):
+        at = pl.ds(pl.multiple_of(s * PIECE, PIECE), PIECE)
+        return pltpu.make_async_remote_copy(
+            src_ref=part.at[u, at], dst_ref=(in_r if right else in_l).at[u, at],
+            send_sem=z_send.at[u, s],
+            recv_sem=(right_recv if right else left_recv).at[u, s],
+            device_id=(row, c + 1 if right else c - 1), device_id_type=MESH)
+
+    barrier = pltpu.get_barrier_semaphore()
+    near = [twin, peer[1], peer[2]]
+    for other in near:
+        pl.semaphore_signal(barrier, inc=1, device_id=(other, c), device_id_type=MESH)
+
+    @pl.when(c > 0)
+    def _():
+        pl.semaphore_signal(barrier, inc=1, device_id=(row, c - 1), device_id_type=MESH)
+
+    @pl.when(c < last)
+    def _():
+        pl.semaphore_signal(barrier, inc=1, device_id=(row, c + 1), device_id_type=MESH)
+
+    def v_copy(i, slot):
+        return pltpu.make_async_copy(
+            v_ref.at[pl.ds(pl.multiple_of(i * STAGE, STAGE), STAGE)], vst.at[slot], v_sem.at[slot])
+
+    v_copy(0, 0).start()
+    v_copy(1, 1).start()
+    line = jnp.where(c > 0, 1, 0) + jnp.where(c < last, 1, 0)
+    pl.semaphore_wait(barrier, len(near) + line)
+
+    for h in range(2):
+        twin_own(h).start()
+    for h in range(2):
+        link_copy(1, h).start()
+
+    v_steps = mrows // STAGE
+
+    def v_body(i, _):
+        slot = i % 2
+        v_copy(i, slot).wait()
+        at = pl.ds(pl.multiple_of(i * STAGE, STAGE), STAGE)
+        val = vst[slot]
+        hi = val.astype(jnp.bfloat16)
+        vh[at, :] = hi
+        vl[at, :] = (val - hi.astype(jnp.float32)).astype(jnp.bfloat16)
+
+        @pl.when(i + 2 < v_steps)
+        def _():
+            v_copy(i + 2, slot).start()
+        return 0
+
+    lax.fori_loop(0, v_steps, v_body, 0)
+
+    ends, total = [], jnp.int32(0)
+    for i in range(blocks - 1):
+        total = total + units_ref[i]
+        ends.append(total * UNIT)
+
+    def block_of(position):
+        got = jnp.int32(0)
+        for end in ends:
+            got = got + jnp.where(position >= end, 1, 0)
+        return got
+
+    def m_copy(src, slot):
+        return pltpu.make_async_copy(src, mst.at[slot], m_sem.at[slot])
+
+    def slot_unit(t, skipped):
+        mixed = 4 + 2 * (t - 4) + jnp.where(skipped == chip_x, 1, 0)
+        mixed = jnp.where(t < 4, t, jnp.where(t < 8, mixed, t + 4))
+        n = jnp.where(skipped == chip, t + 4, jnp.where(skipped == chip_d, t, mixed))
+        q = n // 2
+        return jnp.where(n % 2 == 0, unit_a(q), unit_b(q))
+
+    def forward(u, s, right):
+        z_copy(u, s, right).wait_recv()
+        at = pl.ds(pl.multiple_of(s * PIECE, PIECE), PIECE)
+        local = pltpu.make_async_copy((in_r if right else in_l).at[u, at], held, h_sem)
+        local.start()
+        local.wait()
+        part[u, at, :] = part[u, at, :] + held[...]
+        z_copy(u, s, right).start()
+
+    steps = slots * pieces
+    right_lag, left_lag = (c - 1) * LAG, (last - 1 - c) * LAG
+
+    def handle(first, count):
+        def body(at, _):
+            r, l = at - right_lag, at - left_lag
+            rt, lt = jnp.maximum(r, 0) // pieces, jnp.maximum(l, 0) // pieces
+            ur = slot_unit(jnp.minimum(rt, slots - 1), 0)
+            ul = slot_unit(jnp.minimum(lt, slots - 1), last)
+
+            @pl.when((c > 0) & (c < ur // per_block) & (r >= 0) & (r < steps))
+            def _():
+                forward(ur, r % pieces, True)
+
+            @pl.when((c < last) & (c > ul // per_block) & (l >= 0) & (l < steps))
+            def _():
+                forward(ul, l % pieces, False)
+            return 0
+
+        lax.fori_loop(first, first + count, body, 0)
+
+    early = jnp.where(chip == c, 1, 0)
+
+    def next_chunk(at):
+        return (at + 2 * early) % chunks
+
+    def chunk(at_chunk, _):
+        q, following = next_chunk(at_chunk), next_chunk(at_chunk + 1)
+        ua, ub = unit_a(q), unit_b(q)
+        h = q % 2
+        twin_wait = pltpu.make_async_remote_copy(
+            src_ref=gath.at[ub], dst_ref=gath.at[ub], send_sem=twin_send.at[q],
+            recv_sem=twin_recv.at[q], device_id=(twin, c), device_id_type=MESH)
+        twin_wait.wait_recv()
+
+        @pl.when(q == 3)
+        def _():
+            for hh in range(2):
+                link_copy(3, hh).start()
+
+        @pl.when(q < 2)
+        def _():
+            m_copy(own_cols(h), 0).start()
+
+        @pl.when(q >= 2)
+        def _():
+            m_copy(gath.at[ua], 0).start()
+
+        m_copy(gath.at[ub], 1).start()
+        m_copy(gath.at[ub], 0).wait()
+        m_copy(gath.at[ub], 1).wait()
+
+        sa, sb = block_of(START + ua * LANES), block_of(START + ub * LANES)
+
+        def split(g, _):
+            at = pl.ds(pl.multiple_of(g * UNIT, UNIT), UNIT)
+            mine = block_of(c * inner + g * UNIT)
+            for a, sl in ((0, sa), (1, sb)):
+                keep = jnp.where(mine == sl, jnp.float32(1.0), jnp.float32(0.0))
+                val = mst[a, at, :] * keep
+                hi = val.astype(jnp.bfloat16)
+                mh[at, a * LANES:(a + 1) * LANES] = hi
+                ml[at, a * LANES:(a + 1) * LANES] = (val - hi.astype(jnp.float32)).astype(jnp.bfloat16)
+            return 0
+
+        lax.fori_loop(0, inner // UNIT, split, 0)
+
+        def multiply(s, _):
+            at = pl.ds(pl.multiple_of(s * PIECE, PIECE), PIECE)
+            acc = jnp.dot(vl[at, :], mh[...], preferred_element_type=jnp.float32)
+            acc = jnp.dot(vh[at, :], ml[...], preferred_element_type=jnp.float32) + acc
+            acc = jnp.dot(vh[at, :], mh[...], preferred_element_type=jnp.float32) + acc
+            part[ua, at, :] = acc[:, :LANES]
+            part[ub, at, :] = acc[:, LANES:]
+            for u in (ua, ub):
+                @pl.when((c == 0) & (u // per_block > 0))
+                def _():
+                    z_copy(u, s, True).start()
+
+                @pl.when((c == last) & (u // per_block < last))
+                def _():
+                    z_copy(u, s, False).start()
+            return 0
+
+        lax.fori_loop(0, pieces, multiply, 0)
+
+        @pl.when((following >= 2) & (at_chunk < chunks - 1))
+        def _():
+            link_arrival(following).wait_recv()
+            twin_copy(following).start()
+
+        @pl.when(at_chunk == 1 - early)
+        def _():
+            for hh in range(2):
+                link_copy(2, hh).start()
+
+        @pl.when(at_chunk >= 2)
+        def _():
+            handle((at_chunk - 2) * 2 * pieces, 2 * pieces)
+        return 0
+
+    @pl.when(chip == c)
+    def _():
+        link_arrival(2).wait_recv()
+        twin_copy(2).start()
+
+    lax.fori_loop(0, chunks, chunk, 0)
+    handle(steps, LAG * (cols - 2))
+
+    def landed(u, right):
+        return pltpu.make_async_copy(
+            (in_r if right else in_l).at[u], mst.at[0 if right else 1, pl.ds(0, mrows)],
+            m_sem.at[0 if right else 1])
+
+    def finish(i, _):
+        u = c * per_block + i
+        sides = ((True, c > 0), (False, c < last))
+        for right, there in sides:
+            @pl.when(there)
+            def _():
+                for s in range(pieces):
+                    z_copy(u, s, right).wait_recv()
+                landed(u, right).start()
+        for right, there in sides:
+            @pl.when(there)
+            def _():
+                landed(u, right).wait()
+
+                def add(s, _):
+                    at = pl.ds(pl.multiple_of(s * PIECE, PIECE), PIECE)
+                    part[u, at, :] = part[u, at, :] + mst[0 if right else 1, at, :]
+                    return 0
+
+                lax.fori_loop(0, pieces, add, 0)
+        out_copy(i).start()
+        return 0
+
+    def out_copy(i):
+        return pltpu.make_async_copy(
+            part.at[c * per_block + i],
+            out_ref.at[:, pl.ds(pl.multiple_of(i * LANES, LANES), LANES)], o_sem.at[i])
+
+    lax.fori_loop(0, per_block, finish, 0)
+
+    for h in range(2):
+        twin_own(h).wait_send()
+    for q in range(2, chunks):
+        twin_copy(q).wait_send()
+        link_copy(q // 2, q % 2).wait_send()
+
+    def drain(u, _):
+        @pl.when(u // per_block != c)
+        def _():
+            for s in range(pieces):
+                z_copy(u, s, True).wait_send()
+        return 0
+
+    lax.fori_loop(0, 2 * rows, drain, 0)
+    for i in range(per_block):
+        out_copy(i).wait()
+
+
+def fused(rows, cols, vectors, basis, block_units):
+    mrows, inner = vectors.shape
+    units = 2 * rows
+    pieces = mrows // PIECE
+    f32, bf16 = jnp.float32, jnp.bfloat16
+    any_space = pl.BlockSpec(memory_space=pl.ANY)
+    dma = pltpu.SemaphoreType.DMA
+    flops = 6 * mrows * inner * units * LANES
+    return pl.pallas_call(
+        functools.partial(kernel, rows, cols, block_units.shape[0]),
+        out_shape=[
+            jax.ShapeDtypeStruct((mrows, units * LANES // cols), f32),
+            jax.ShapeDtypeStruct((units, inner, LANES), f32),
+            jax.ShapeDtypeStruct((units, mrows, LANES), f32),
+            jax.ShapeDtypeStruct((units, mrows, LANES), f32),
+        ],
+        in_specs=[pl.BlockSpec(memory_space=pltpu.SMEM), any_space, any_space],
+        out_specs=[any_space] * 4,
+        scratch_shapes=[
+            pltpu.VMEM((mrows, inner), bf16),
+            pltpu.VMEM((mrows, inner), bf16),
+            pltpu.VMEM((units, mrows, LANES), f32),
+            pltpu.VMEM((2, STAGE, inner), f32),
+            pltpu.VMEM((2, inner, LANES), f32),
+            pltpu.VMEM((inner, 2 * LANES), bf16),
+            pltpu.VMEM((inner, 2 * LANES), bf16),
+            pltpu.VMEM((PIECE, LANES), f32),
+            dma((2,)), dma((2,)), dma, dma((units // cols,)),
+            dma((rows,)), dma((rows,)), dma((rows,)), dma((rows,)),
+            dma((units, pieces)), dma((units, pieces)), dma((units, pieces)),
+        ],
+        compiler_params=pltpu.CompilerParams(
+            collective_id=0, has_side_effects=True, vmem_limit_bytes=VMEM_BYTES),
+        cost_estimate=pl.CostEstimate(flops=flops, bytes_accessed=4 * mrows * inner, transcendentals=0),
+    )(block_units, vectors, basis)[0]
+
+
 def solution(mesh):
+    rows, cols = mesh.shape["row"], mesh.shape["col"]
+
+    def shards(vectors, basis, block_units):
+        fits = rows // 2 == cols == 4 and basis.shape[1] == 2 * LANES
+        if fits and vectors.shape[0] % PIECE == 0 and vectors.shape[1] % UNIT == 0:
+            return fused(rows, cols, vectors, basis, block_units)
+        return plain(vectors, basis, block_units)
+
     in_specs = (P("row", "col"), P("col", "row"), P())
-    out_specs = P("row", "col")
-    return jax.shard_map(shards, mesh=mesh, in_specs=in_specs, out_specs=out_specs, check_vma=False)
+    return jax.shard_map(
+        shards, mesh=mesh, in_specs=in_specs, out_specs=P("row", "col"), check_vma=False)

time: 529 us -> 373 us (0.71)
  Pallas kernels: 0 us -> 366 us
  waiting for transfers between devices: 273 us -> 0 us
  matrix products: 222 us -> 0 us
  between operations: 13.2 us -> 0.01 us
  other arithmetic: 7.3 us -> 0 us
  local copies, waits for them, and re-layouts: 11.1 us -> 4.64 us
    pallas_call x0 -> x1, Pallas kernels: none -> 366 us  [fused(): pl.pallas_call(functools.partial(kernel, rows, cols, block_units.shape[0]...]
    dot_general x2 -> x0, matrix products: 222 us -> none  [shards(): jnp.dot(vectors, piece, precision=lax.Precision.HIGH, preferred_element_t...]
    reduce_scatter x2 -> x0, waiting for transfers between devices: 179 us -> none  [shards(): sums.append(lax.psum_scatter(part, 'col', scatter_dimension=1, tiled=True))]
    all_gather x2 -> x0, waiting for transfers between devices: 93.1 us -> none  [shards(): lax.all_gather(masked[:, at:at + step], 'row', axis=1, tiled=True)]
    slice x4 -> x0, local copies, waits for them, and re-layouts: 5.75 us -> none  [the longest x2 3.43 us: shards(): one[:, g * step:(g + 1) * step]]
    concatenate x1 -> x0, local copies, waits for them, and re-layouts: 5.34 us -> none  [shards(): jnp.concatenate([one[:, g * step:(g + 1) * step] for g in range(groups) f...]
  transfers between devices with their start and end apart: 4 -> 0, of which waited for: 3 -> 0; matrix products, arithmetic and copies ran while one was open for 42% -> 0% of each run, Pallas kernels for 0% -> 0%
where the time goes in v1:
time: 373 us; the launch traced here: 370 us
  Pallas kernels  366 us (98%)
  local copies, waits for them, and re-layouts  4.64 us (1%)
    pallas_call x1, Pallas kernels, fused(): pl.pallas_call(functools.partial(kernel, rows, cols, block_units.shape[0]...  366 us

profile of v1, /device:TPU:7, one launch (start us, length us, event | category | flops | bytes accessed | tf_op | source)
XLA Modules:
  0.0 370.4 jit_solution(15102290683928201614)
XLA Ops:
  0.0 365.8 %shard_map.37 = (f32[2048,512]{1,0:T(8,128)}, f32[16,4096,128]{2,1,0:T(8,128)}, f32[16,2048,128]{2,1,0:T(8,128)}, f32[16,2048,128]{2,1,0:T(8,128)}) custom-call(s32[8]{0:T(128)} %units_ref.1, f32[2048,4096]{1,0:T(8,128)} %v_ref.1, f32[4096,256]{1,0:T(8,128)} %b_ref.1), custom_call_target="tpu_custom_call" | custom-call | flops 103079215104 | bytes 33554432 | tf_op jit(solution)/shard_map/pallas_call | solution.py:384
  365.8 4.6 %copy.5 = f32[2048,512]{1,0:T(8,128)} copy(f32[2048,512]{1,0:T(8,128)} %get-tuple-element.6) | data formatting | bytes 8388608
